TPU v7x, 256 devices: a 8x8x2 block of a 8x8x16 slice. The times are simulated.
256 devices in a mesh: groups: 2 (over z), tensor: 64 (over x, y), seq: 2 (over core).
Axes of the slice: x: 8, y: 8, z: 2, core: 2. Of those that a mesh axis runs over, the one named last changes fastest.
The devices are a block of a 8x8x16 slice.
Arguments:
- heads_out: bfloat16 [1024, 4096], P(('groups', 'seq'), 'tensor'), parts along dimension 0, may hold values from -6 to 6
- stream_in: bfloat16 [1024, 8192], P(('groups', 'seq', 'tensor')), parts along dimension 0, may hold values from -40 to 40, as said below
- proj_levels: bfloat16 [4096, 8192], P('tensor'), may hold values from -8 to 7, as said below
- proj_scale: float32 [8192], replicated, may hold values from 0.001703125 to 0.006796875
- norm_gain: float32 [8192], replicated, may hold values from 0.25 to 1.75
- gate_levels: bfloat16 [8192, 14336], P(None, 'tensor'), may hold values from -8 to 7, as said below
- gate_scale: float32 [14336], P('tensor'), may hold values from 0.0012153398 to 0.004861359
- gate_index: int32 [64, 8], P('tensor'), may hold values from 0 to 223, as said below
- gate_extra: bfloat16 [8192, 512], P(None, 'tensor'), may hold values from -0.29882812 to 0.29882812
- up_levels: bfloat16 [8192, 14336], P(None, 'tensor'), may hold values from -8 to 7, as said below
- up_scale: float32 [14336], P('tensor'), may hold values from 0.0012153398 to 0.004861359
- up_index: int32 [64, 8], P('tensor'), may hold values from 0 to 223, as said below
- up_extra: bfloat16 [8192, 512], P(None, 'tensor'), may hold values from -0.29882812 to 0.29882812
- down_levels: bfloat16 [14336, 8192], P('tensor'), may hold values from -8 to 7, as said below
- down_scale: float32 [8192], replicated, may hold values from 0.0009020067 to 0.003591323
- down_index: int32 [64, 8], P('tensor'), may hold values from 0 to 8191, as said below
- down_extra: bfloat16 [14336, 8], P('tensor'), may hold values from -0.29882812 to 0.29882812
Outputs:
- stream_out: bfloat16 [1024, 8192], P(('groups', 'seq', 'tensor')), parts along dimension 0
There are 2 independent parts, one for each index of `groups`. A program takes and returns all parts, laid end to end along the dimension named above; an argument that names none is the same for every part. Nothing has to cross between parts.
Inputs may be any that keep to these rules, and one draw needn't show every extreme that they name: stream_in has rows and columns of differing scales. `proj_levels`: integer values. `gate_levels`: integer values. `up_levels`: integer values. `down_levels`: integer values. `gate_index`: each row holds 8 different numbers. `up_index`: each row holds 8 different numbers. `down_index`: each row holds 8 different numbers.
All inputs are finite; a program needn't handle non-finite values.
Results may differ from a plain program's by a relative error of at most 0.0055.
Values may be sent and summed in bfloat16 or wider, within the bound.
A program may use at most 128 MiB of HBM per device.

v0:
```python
import jax
import jax.numpy as jnp
from jax import lax
from jax.sharding import Mesh
from jax.sharding import PartitionSpec as P

TENSOR = ("tensor_0", "tensor_1")
GROUPS_SEQ_TENSOR = ("groups", "seq", "tensor_0", "tensor_1")


def own_rows_2(running, axes):
    for axis in axes:
        running = lax.psum_scatter(running, axis, scatter_dimension=0, tiled=True)
    return running


def rms_norm(mixed, norm_gain):
    mean_sq = jnp.mean(mixed * mixed, axis=-1, keepdims=True)
    return (mixed * lax.rsqrt(mean_sq + 1e-05) * norm_gain).astype(jnp.bfloat16)


def picker(index_row, width):
    return (index_row[:, None] == jnp.arange(width, dtype=jnp.int32)[None, :]).astype(jnp.float32)


def project(rows_in, levels, scale, extra, chosen):
    base = jnp.dot(rows_in, levels, preferred_element_type=jnp.float32)
    added = jnp.dot(rows_in, extra, preferred_element_type=jnp.float32)
    return base * scale + jnp.dot(added, chosen, precision=lax.Precision.HIGHEST)


def local(
    heads_out,
    stream_in,
    proj_levels,
    proj_scale,
    norm_gain,
    gate_levels,
    gate_scale,
    gate_index,
    gate_extra,
    up_levels,
    up_scale,
    up_index,
    up_extra,
    down_levels,
    down_scale,
    down_index,
    down_extra,
):
    shard_width = gate_levels.shape[1]
    model_width = proj_levels.shape[1]
    gate_pick = picker(gate_index[0], shard_width)
    up_pick = picker(up_index[0], shard_width)
    down_pick = picker(down_index[0], model_width)
    taken = heads_out
    proj = own_rows_2(
        jnp.dot(taken, proj_levels, preferred_element_type=jnp.float32) * proj_scale, TENSOR
    )
    mixed = stream_in.astype(jnp.float32) + proj
    normed = rms_norm(mixed, norm_gain)
    normed_rows = lax.all_gather(normed, TENSOR, axis=0, tiled=True)
    gate = project(normed_rows, gate_levels, gate_scale, gate_extra, gate_pick)
    up = project(normed_rows, up_levels, up_scale, up_extra, up_pick)
    hidden = (jax.nn.silu(gate) * up).astype(jnp.bfloat16)
    taken = hidden
    down = own_rows_2(project(taken, down_levels, down_scale, down_extra, down_pick), TENSOR)
    return (mixed + down).astype(jnp.bfloat16)


def solution(mesh):
    torus = Mesh(
        mesh.devices.reshape(mesh.shape["groups"], 8, 8, mesh.shape["seq"]),
        ("groups", "tensor_0", "tensor_1", "seq"),
    )
    return jax.shard_map(
        local,
        mesh=torus,
        in_specs=(
            P(("groups", "seq"), TENSOR),
            P(GROUPS_SEQ_TENSOR, None),
            P(TENSOR, None),
            P(),
            P(),
            P(None, TENSOR),
            P(TENSOR),
            P(TENSOR, None),
            P(None, TENSOR),
            P(None, TENSOR),
            P(TENSOR),
            P(TENSOR, None),
            P(None, TENSOR),
            P(TENSOR, None),
            P(),
            P(TENSOR, None),
            P(TENSOR, None),
        ),
        out_specs=P(GROUPS_SEQ_TENSOR, None),
        check_vma=False,
    )
```

profile of v0, /device:TPU:514, one launch (start us, length us, event | category | flops | bytes accessed | tf_op | source)
XLA Modules:
  0.0 497.5 jit_solution(14102043110908546794)
XLA Ops:
  6.5 0.0 copy-start
  6.6 0.0 reduce-scatter.3.cloned.1.call-start
  6.6 1.2 copy-done
  7.8 5.3 %convolution_multiply_fusion.1 = f32[256,8192]{1,0:T(8,128)} fusion(bf16[256,64]{0,1:T(8,128)(2,1)} %param.17, bf16[64,8192]{1,0:T(8,128)(2,1)S(1)} %copy-done, f32[8192]{0:T(1024)} %param.20), kind=kOutput, calls=%fused_computation.2 | convolution fusion | flops 270532608 | bytes 9502720 | tf_op jit(solution)/shard_map/dot_general | solution.py:58
  13.1 0.0 copy-start.16
  13.1 0.0 copy-start.3
  13.1 0.0 copy-start.5
  13.1 0.1 reduce-scatter.3.cloned.1.call-update
  13.1 0.1 all-reduce.5.cloned.1.call-start
  13.2 112.5 %reduce-scatter.3.cloned.1.call-done = f32[32,8192]{1,0:T(8,128)} async-done(((f32[256,8192]{1,0:T(8,128)}), f32[32,8192]{1,0:T(8,128)}) %reduce-scatter.3.cloned.1.call-update) | async-done | bytes 1048592 | tf_op jit(solution)/shard_map/reduce_scatter | solution.py:13
  125.7 0.1 all-reduce.5.cloned.1.call-update
  125.7 0.1 all-gather.3.cloned.1.call-start
  125.8 0.0 copy-done.16
  125.8 0.6 dynamic-slice
  127.0 80.4 %all-reduce.5.cloned.1.call-done = f32[32,8192]{1,0:T(8,128)} async-done(((f32[32,8192]{1,0:T(8,128)}), f32[32,8192]{1,0:T(8,128)}) %all-reduce.5.cloned.1.call-update) | async-done | bytes 1048592
  207.4 0.0 copy-done.3
  207.4 1.1 multiply_reduce_fusion
  208.6 0.0 copy-done.5
  208.6 1.7 fusion.4
  210.3 0.1 all-gather.3.cloned.1.call-update
  210.3 0.0 copy-start.11
  210.3 0.1 reduce-scatter.5.cloned.1.call-start
  210.4 81.7 %all-gather.3.cloned.1.call-done = bf16[64,4,8192]{2,1,0:T(4,128)(2,1)} async-done(((bf16[1,4,8192]{2,1,0:T(4,128)(2,1)}), bf16[64,4,8192]{2,1,0:T(4,128)(2,1)}) %all-gather.3.cloned.1.call-update) | async-done | bytes 4194320 | tf_op jit(solution)/shard_map/all_gather | solution.py:62
  292.1 0.0 copy-start.12
  292.1 7.0 %reshape.17 = bf16[256,8192]{1,0:T(8,128)(2,1)} reshape(bf16[64,4,8192]{2,1,0:T(4,128)(2,1)} %all-gather.3.cloned.1.call-done) | data formatting | bytes 8388608
  299.1 0.0 copy-done.11
  299.1 0.0 copy-start.1
  299.1 0.0 copy-start.9
  299.1 0.0 copy-start.13
  299.1 3.6 fusion.8
  302.6 0.0 copy-done.12
  302.6 0.0 copy-done.1
  302.7 1.2 fusion.7
  303.9 0.0 copy-done.9
  303.9 0.0 copy-done.13
  303.9 0.0 copy-start.10
  303.9 0.0 copy-start.14
  303.9 1.6 convolution_multiply_fusion.2
  305.5 0.4 copy-done.10
  305.9 0.0 copy-done.14
  305.9 0.0 copy-start.8
  305.9 0.0 copy-start.15
  305.9 0.0 copy-start.6
  305.9 0.0 copy-start.2
  306.0 0.0 copy-start.4
  306.0 1.4 convolution_multiply_fusion.3
  307.4 0.0 copy-done.8
  307.4 0.4 convolution_add_fusion.2
  307.8 0.0 copy-done.15
  307.8 0.4 fusion.1
  308.1 0.0 copy-done.6
  308.1 0.2 fusion.9
  308.4 0.0 copy-done.2
  308.4 0.0 copy-done.4
  308.4 0.0 copy-start.7
  308.4 1.3 convolution_multiply_fusion
  309.7 0.0 copy-done.7
  309.7 5.9 %convolution_add_fusion = f32[256,8192]{1,0:T(8,128)} fusion(f32[256,8192]{1,0:T(8,128)S(1)} %convolution_multiply_fusion, f32[256,8]{1,0:T(8,128)S(1)} %fusion.9, s32[8]{0:T(128)S(1)} %bitcast.23), kind=kOutput, calls=%fused_computation | convolution fusion | flops 203489280 | bytes 16785440 | tf_op jit(solution)/shard_map/dot_general | solution.py:29
  315.6 0.1 reduce-scatter.5.cloned.1.call-update
  315.6 0.1 all-reduce.7.cloned.1.call-start
  315.7 91.8 %reduce-scatter.5.cloned.1.call-done = f32[32,8192]{1,0:T(8,128)} async-done(((f32[256,8192]{1,0:T(8,128)}), f32[32,8192]{1,0:T(8,128)}) %reduce-scatter.5.cloned.1.call-update) | async-done | bytes 1048592 | tf_op jit(solution)/shard_map/reduce_scatter | solution.py:13
  407.5 0.1 all-reduce.7.cloned.1.call-update
  407.6 81.7 %all-reduce.7.cloned.1.call-done = f32[32,8192]{1,0:T(8,128)} async-done(((f32[32,8192]{1,0:T(8,128)}), f32[32,8192]{1,0:T(8,128)}) %all-reduce.7.cloned.1.call-update) | async-done | bytes 1048592
  489.2 1.7 fusion.2
  (1 shorter events, 0.0 us)
Async XLA Ops:
  6.5 1.2 copy-start
  6.6 119.1 %reduce-scatter.3.cloned.1.call-start = ((), (), s32[]{:S(2)}) async-start(), calls=%async_computation.2 | async-start | bytes 9437184 | tf_op jit(solution)/shard_map/reduce_scatter | solution.py:13
  13.1 112.7 %copy-start.16 = (u32[256]{0:T(256)S(1)}, u32[256]{0:T(256)}, u32[]{:S(2)}) copy-start(u32[256]{0:T(256)} %constant.24) | copy-start | bytes 3076
  13.1 194.4 %copy-start.3 = (bf16[4,8192]{1,0:T(4,128)(2,1)S(1)}, bf16[4,8192]{1,0:T(4,128)(2,1)}, u32[]{:S(2)}) copy-start(bf16[4,8192]{1,0:T(4,128)(2,1)} %param.18) | copy-start | bytes 196612
  13.1 195.5 %copy-start.5 = (f32[8192]{0:T(1024)S(1)}, f32[8192]{0:T(1024)}, u32[]{:S(2)}) copy-start(f32[8192]{0:T(1024)} %param.21) | copy-start | bytes 98308
  13.1 194.3 %all-reduce.5.cloned.1.call-start = ((), (), s32[]{:S(2)}) async-start(), calls=%async_computation.5 | async-start | bytes 2097152
  125.7 166.3 %all-gather.3.cloned.1.call-start = ((), (), s32[]{:S(2)}) async-start(), calls=%async_computation.4 | async-start | bytes 4259840 | tf_op jit(solution)/shard_map/all_gather | solution.py:62
  210.3 88.7 %copy-start.11 = (bf16[8192,8]{0,1:T(8,128)(2,1)S(1)}, bf16[8192,8]{0,1:T(8,128)(2,1)}, u32[]{:S(2)}) copy-start(bf16[8192,8]{0,1:T(8,128)(2,1)} %param.29) | copy-start | bytes 393220
  210.3 197.2 %reduce-scatter.5.cloned.1.call-start = ((), (), s32[]{:S(2)}) async-start(), calls=%async_computation.3 | async-start | bytes 9437184 | tf_op jit(solution)/shard_map/reduce_scatter | solution.py:13
  292.1 10.6 %copy-start.12 = (bf16[8192,8]{0,1:T(8,128)(2,1)S(1)}, bf16[8192,8]{0,1:T(8,128)(2,1)}, u32[]{:S(2)}) copy-start(bf16[8192,8]{0,1:T(8,128)(2,1)} %param.25) | copy-start | bytes 393220
  299.1 3.6 copy-start.1
  299.1 4.8 copy-start.9
  299.1 4.8 copy-start.13
  303.9 2.0 copy-start.10
  303.9 2.0 copy-start.14
  305.9 1.4 copy-start.8
  305.9 1.8 copy-start.15
  305.9 2.2 copy-start.6
  305.9 2.4 copy-start.2
  306.0 2.4 copy-start.4
  308.4 1.3 copy-start.7
  315.6 173.6 %all-reduce.7.cloned.1.call-start = ((), (), s32[]{:S(2)}) async-start(), calls=%async_computation.6 | async-start | bytes 2097152
Sparse Core Ops, SparseCore 0:
  13.2 112.3 reduce-scatter.2
  128.0 79.3 all-reduce.4
  210.4 81.5 all-gather.2
  315.7 91.7 reduce-scatter.4
  409.7 79.4 all-reduce.6
where the time goes:
time: 498 us
  waiting for transfers between devices  448 us (90%)
  matrix products  21.1 us (4%)
  between operations  14 us (3%)
  local copies, waits for them, and re-layouts  9.28 us (2%)
    reduce_scatter x2, waiting for transfers between devices, own_rows_2(): running = lax.psum_scatter(running, axis, scatter_dimension=0, tiled=True)  204 us
    unnamed x7, waiting for transfers between devices  162 us
    all_gather x1, waiting for transfers between devices, local(): normed_rows = lax.all_gather(normed, TENSOR, axis=0, tiled=True)  81.7 us
  transfers between devices with their start and end apart: 5, of which 5 were waited for; matrix products, arithmetic and copies ran while one was open for 0% of the time, Pallas kernels for 0%

commit v1 on v0

--- a/solution.py
+++ b/solution.py
@@ -59,7 +59,9 @@
     )
     mixed = stream_in.astype(jnp.float32) + proj
     normed = rms_norm(mixed, norm_gain)
-    normed_rows = lax.all_gather(normed, TENSOR, axis=0, tiled=True)
+    normed_rows = jnp.concatenate(
+        lax.all_to_all(jnp.stack([normed] * lax.axis_size(TENSOR)), TENSOR, 0, 0), axis=0
+    )
     gate = project(normed_rows, gate_levels, gate_scale, gate_extra, gate_pick)
     up = project(normed_rows, up_levels, up_scale, up_extra, up_pick)
     hidden = (jax.nn.silu(gate) * up).astype(jnp.bfloat16)

time: 498 us -> 524 us (1.052)
  blocking collectives: 0 us -> 103 us
  waiting for transfers between devices: 448 us -> 370 us
    all_to_all x0 -> x1, blocking collectives: none -> 103 us  [local(): lax.all_to_all(jnp.stack([normed] * lax.axis_size(TENSOR)), TENSOR, 0, 0)]
    all_gather x1 -> x0, waiting for transfers between devices: 81.7 us -> none  [local(): normed_rows = lax.all_gather(normed, TENSOR, axis=0, tiled=True)]
    unnamed x36 -> x35, local copies, waits for them, and re-layouts: 9.28 us -> 2.28 us
    reshape x0 -> x1, local copies, waits for them, and re-layouts: none -> 6.99 us  [local(): jnp.concatenate(lax.all_to_all(jnp.stack([normed] * lax.axis_size(TENSOR)...]
    unnamed x7 -> x6, waiting for transfers between devices: 162 us -> 162 us
  transfers between devices with their start and end apart: 5 -> 4, of which waited for: 5 -> 4; matrix products, arithmetic and copies ran while one was open for 0% -> 0% of each run, Pallas kernels for 0% -> 0%
where the time goes in v1:
time: 524 us; the launch traced here: 523 us
  waiting for transfers between devices  370 us (71%)
  blocking collectives  103 us (20%)
  matrix products  21.1 us (4%)
  between operations  14 us (3%)
  local copies, waits for them, and re-layouts  11.3 us (2%)
    reduce_scatter x2, waiting for transfers between devices, own_rows_2(): running = lax.psum_scatter(running, axis, scatter_dimension=0, tiled=True)  208 us
    unnamed x6, waiting for transfers between devices  162 us
    all_to_all x1, blocking collectives, local(): lax.all_to_all(jnp.stack([normed] * lax.axis_size(TENSOR)), TENSOR, 0, 0)  103 us
  transfers between devices with their start and end apart: 4, of which 4 were waited for; matrix products, arithmetic and copies ran while one was open for 0% of the time, Pallas kernels for 0%

profile of v1, /device:TPU:514, one launch (start us, length us, event | category | flops | bytes accessed | tf_op | source)
XLA Modules:
  0.0 523.1 jit_solution(14027163551749863295)
XLA Ops:
  6.5 0.0 copy-start
  6.6 0.0 reduce-scatter.3.cloned.1.call-start
  6.6 1.2 copy-done
  7.8 5.3 %convolution_multiply_fusion.1 = f32[256,8192]{1,0:T(8,128)} fusion(bf16[256,64]{0,1:T(8,128)(2,1)} %param.17, bf16[64,8192]{1,0:T(8,128)(2,1)S(1)} %copy-done, f32[8192]{0:T(1024)} %param.20), kind=kOutput, calls=%fused_computation.2 | convolution fusion | flops 270532608 | bytes 9502720 | tf_op jit(solution)/shard_map/dot_general | solution.py:58
  13.0 0.0 copy-start.16
  13.0 0.0 copy-start.3
  13.0 0.0 copy-start.5
  13.0 0.1 reduce-scatter.3.cloned.1.call-update
  13.1 0.1 all-reduce.5.cloned.1.call-start
  13.2 112.5 %reduce-scatter.3.cloned.1.call-done = f32[32,8192]{1,0:T(8,128)} async-done(((f32[256,8192]{1,0:T(8,128)}), f32[32,8192]{1,0:T(8,128)}) %reduce-scatter.3.cloned.1.call-update) | async-done | bytes 1048592 | tf_op jit(solution)/shard_map/reduce_scatter | solution.py:13
  125.6 0.1 all-reduce.5.cloned.1.call-update
  125.7 0.1 reduce-scatter.5.cloned.1.call-start
  125.8 0.0 copy-done.16
  125.8 0.6 dynamic-slice
  127.0 80.5 %all-reduce.5.cloned.1.call-done = f32[32,8192]{1,0:T(8,128)} async-done(((f32[32,8192]{1,0:T(8,128)}), f32[32,8192]{1,0:T(8,128)}) %all-reduce.5.cloned.1.call-update) | async-done | bytes 1048592
  207.5 0.0 copy-done.3
  207.5 1.1 multiply_reduce_fusion
  208.6 0.0 copy-done.5
  208.6 1.1 multiply_convert_fusion
  209.7 2.0 stack.2
  211.7 102.8 %all_to_all.5 = bf16[64,4,8192]{2,1,0:T(4,128)(2,1)} all-to-all(bf16[64,4,8192]{2,1,0:T(4,128)(2,1)S(1)} %stack.2), channel_id=1, replica_groups=mesh['groups'=2,'tensor_0'=8,'tensor_1'=8,'seq'=2] {'tensor_0','tensor_1'}, dimensions={0} | all-to-all | bytes 8388608 | tf_op jit(solution)/shard_map/all_to_all | solution.py:63
  314.6 0.0 copy-start.11
  314.6 0.0 copy-start.12
  314.6 7.0 %reshape.21 = bf16[256,8192]{1,0:T(8,128)(2,1)} reshape(bf16[64,4,8192]{2,1,0:T(4,128)(2,1)} %all_to_all.5) | data formatting | bytes 8388608 | tf_op jit(solution)/shard_map/reshape | solution.py:62
  321.5 0.0 copy-done.11
  321.5 0.0 copy-start.1
  321.5 0.0 copy-start.9
  321.6 0.0 copy-start.13
  321.6 3.6 fusion.7
  325.1 0.0 copy-done.12
  325.1 0.0 copy-done.1
  325.1 1.2 fusion.6
  326.4 0.0 copy-done.9
  326.4 0.0 copy-done.13
  326.4 0.0 copy-start.10
  326.4 0.0 copy-start.14
  326.4 1.6 convolution_multiply_fusion.2
  328.0 0.4 copy-done.10
  328.4 0.0 copy-done.14
  328.4 0.0 copy-start.8
  328.4 0.0 copy-start.15
  328.4 0.0 copy-start.6
  328.4 0.0 copy-start.2
  328.4 0.0 copy-start.4
  328.5 1.4 convolution_multiply_fusion.3
  329.9 0.0 copy-done.8
  329.9 0.4 convolution_add_fusion.2
  330.3 0.0 copy-done.15
  330.3 0.4 fusion.1
  330.6 0.0 copy-done.6
  330.6 0.2 fusion.8
  330.9 0.0 copy-done.2
  330.9 0.0 copy-done.4
  330.9 0.0 copy-start.7
  330.9 1.3 convolution_multiply_fusion
  332.2 0.0 copy-done.7
  332.2 5.9 %convolution_add_fusion = f32[256,8192]{1,0:T(8,128)} fusion(f32[256,8192]{1,0:T(8,128)S(1)} %convolution_multiply_fusion, f32[256,8]{1,0:T(8,128)S(1)} %fusion.8, s32[8]{0:T(128)S(1)} %bitcast.21), kind=kOutput, calls=%fused_computation | convolution fusion | flops 203489280 | bytes 16785440 | tf_op jit(solution)/shard_map/dot_general | solution.py:29
  338.1 0.1 reduce-scatter.5.cloned.1.call-update
  338.1 0.1 all-reduce.7.cloned.1.call-start
  338.2 95.0 %reduce-scatter.5.cloned.1.call-done = f32[32,8192]{1,0:T(8,128)} async-done(((f32[256,8192]{1,0:T(8,128)}), f32[32,8192]{1,0:T(8,128)}) %reduce-scatter.5.cloned.1.call-update) | async-done | bytes 1048592 | tf_op jit(solution)/shard_map/reduce_scatter | solution.py:13
  433.2 0.1 all-reduce.7.cloned.1.call-update
  433.3 81.6 %all-reduce.7.cloned.1.call-done = f32[32,8192]{1,0:T(8,128)} async-done(((f32[32,8192]{1,0:T(8,128)}), f32[32,8192]{1,0:T(8,128)}) %all-reduce.7.cloned.1.call-update) | async-done | bytes 1048592
  514.9 1.7 fusion.2
  (1 shorter events, 0.0 us)
Async XLA Ops:
  6.5 1.2 copy-start
  6.6 119.1 %reduce-scatter.3.cloned.1.call-start = ((), (), s32[]{:S(2)}) async-start(), calls=%async_computation.3 | async-start | bytes 9437184 | tf_op jit(solution)/shard_map/reduce_scatter | solution.py:13
  13.0 112.7 %copy-start.16 = (u32[256]{0:T(256)S(1)}, u32[256]{0:T(256)}, u32[]{:S(2)}) copy-start(u32[256]{0:T(256)} %constant.24) | copy-start | bytes 3076
  13.0 194.4 %copy-start.3 = (bf16[4,8192]{1,0:T(4,128)(2,1)S(1)}, bf16[4,8192]{1,0:T(4,128)(2,1)}, u32[]{:S(2)}) copy-start(bf16[4,8192]{1,0:T(4,128)(2,1)} %param.18) | copy-start | bytes 196612
  13.0 195.6 %copy-start.5 = (f32[8192]{0:T(1024)S(1)}, f32[8192]{0:T(1024)}, u32[]{:S(2)}) copy-start(f32[8192]{0:T(1024)} %param.21) | copy-start | bytes 98308
  13.1 194.4 %all-reduce.5.cloned.1.call-start = ((), (), s32[]{:S(2)}) async-start(), calls=%async_computation.5 | async-start | bytes 2097152
  125.7 307.5 %reduce-scatter.5.cloned.1.call-start = ((), (), s32[]{:S(2)}) async-start(), calls=%async_computation.4 | async-start | bytes 9437184 | tf_op jit(solution)/shard_map/reduce_scatter | solution.py:13
  314.6 7.0 %copy-start.11 = (bf16[8192,8]{0,1:T(8,128)(2,1)S(1)}, bf16[8192,8]{0,1:T(8,128)(2,1)}, u32[]{:S(2)}) copy-start(bf16[8192,8]{0,1:T(8,128)(2,1)} %param.29) | copy-start | bytes 393220
  314.6 10.6 %copy-start.12 = (bf16[8192,8]{0,1:T(8,128)(2,1)S(1)}, bf16[8192,8]{0,1:T(8,128)(2,1)}, u32[]{:S(2)}) copy-start(bf16[8192,8]{0,1:T(8,128)(2,1)} %param.25) | copy-start | bytes 393220
  321.5 3.6 copy-start.1
  321.5 4.8 copy-start.9
  321.6 4.8 copy-start.13
  326.4 2.0 copy-start.10
  326.4 2.0 copy-start.14
  328.4 1.4 copy-start.8
  328.4 1.8 copy-start.15
  328.4 2.2 copy-start.6
  328.4 2.4 copy-start.2
  328.4 2.4 copy-start.4
  330.9 1.3 copy-start.7
  338.1 176.8 %all-reduce.7.cloned.1.call-start = ((), (), s32[]{:S(2)}) async-start(), calls=%async_computation.6 | async-start | bytes 2097152
Sparse Core Ops, SparseCore 0:
  13.2 112.3 reduce-scatter.2
  128.0 79.4 all-reduce.4
  338.2 94.9 reduce-scatter.4
  435.5 79.3 all-reduce.6
